TPU v7x, 32 devices: a whole 2x2x4 slice. The times are simulated.
32 devices in a mesh: blk: 16 (over z, y, core), tp: 2 (over x).
Axes of the slice: x: 2, y: 2, z: 4, core: 2. Of those that a mesh axis runs over, the one named last changes fastest.
Arguments:
- dec_states: bfloat16 [4096, 5120], P('blk', 'tp'), may hold values from -200 to 200
- norm_gain: float32 [5120], replicated, may hold values from 0.1 to 1.9
- query_weight: bfloat16 [5120, 768], P(None, 'tp'), may hold values from -0.078125 to 0.078125
- out_weight: bfloat16 [768, 5120], P('tp'), may hold values from -0.21875 to 0.21875
- enc_keys: bfloat16 [6144, 768], P('blk', 'tp'), may hold values from -1000 to 1000
- enc_values: bfloat16 [6144, 768], P('blk', 'tp'), may hold values from -6 to 6
Outputs:
- attn_out: bfloat16 [4096, 5120], P('blk', 'tp')
All inputs are finite; a program needn't handle non-finite values.
Results may differ from a plain program's by a relative error of at most 0.034.
Values may be sent and summed in bfloat16 or wider, within the bound.
A program may use at most 128 MiB of HBM per device.

v0:
```python
import math
import jax
import jax.numpy as jnp
from jax import lax
from jax.sharding import PartitionSpec as P

HEAD_DIM = 128
NORM_EPS = 1e-06


def block_rows(total_rows, shard_rows, limit):
    shards = total_rows // shard_rows
    chosen = 1
    for count_try in range(1, shards + 1):
        if shards % count_try == 0 and count_try * shard_rows <= limit:
            chosen = count_try
    return chosen * shard_rows


def per_device(dec_states, norm_gain, query_weight, out_weight, enc_keys, enc_values):
    heads = query_weight.shape[1] // HEAD_DIM
    q_rows = dec_states.shape[0]
    score_scale = 1.0 / math.sqrt(HEAD_DIM)
    states = lax.all_gather(dec_states, "tp", axis=1, tiled=True).astype(jnp.float32)
    mean_sq = jnp.mean(states * states, axis=1, keepdims=True)
    normed = (states * lax.rsqrt(mean_sq + NORM_EPS) * norm_gain).astype(jnp.bfloat16)
    queries = jnp.dot(normed, query_weight, preferred_element_type=jnp.float32).astype(jnp.bfloat16)
    query_heads = queries.reshape(q_rows, heads, HEAD_DIM)
    shard_rows = enc_keys.shape[0]
    start_state = (
        jnp.full((heads, q_rows), -1e30, jnp.float32),
        jnp.zeros((heads, q_rows), jnp.float32),
        jnp.zeros((heads, q_rows, HEAD_DIM), jnp.float32),
    )
    key_rows = lax.all_gather(enc_keys, "blk", axis=0, tiled=True)
    value_rows = lax.all_gather(enc_values, "blk", axis=0, tiled=True)
    count = key_rows.shape[0]
    width_rows = block_rows(count, shard_rows, 1536)
    key_blocks = key_rows.reshape(count // width_rows, width_rows, heads, HEAD_DIM)
    value_blocks = value_rows.reshape(count // width_rows, width_rows, heads, HEAD_DIM)

    def step_block(state, blocks):
        row_max, row_sum, summed = state
        key_block, value_block = blocks
        scores = (
            jnp.einsum("qhd,khd->hqk", query_heads, key_block, preferred_element_type=jnp.float32)
            * score_scale
        )
        new_max = jnp.maximum(row_max, jnp.max(scores, axis=2))
        factor = jnp.exp(row_max - new_max)
        exp_scores = jnp.exp(scores - new_max[:, :, None])
        new_sum = row_sum * factor + jnp.sum(exp_scores, axis=2)
        mixed = jnp.einsum(
            "hqk,khd->hqd",
            exp_scores.astype(jnp.bfloat16),
            value_block,
            preferred_element_type=jnp.float32,
        )
        return ((new_max, new_sum, summed * factor[:, :, None] + mixed), None)

    result, unused = lax.scan(step_block, start_state, (key_blocks, value_blocks))
    row_max, row_sum, summed = result
    attended = (
        (summed / row_sum[:, :, None])
        .transpose(1, 0, 2)
        .reshape(q_rows, heads * HEAD_DIM)
        .astype(jnp.bfloat16)
    )
    partial_out = jnp.dot(attended, out_weight, preferred_element_type=jnp.float32)
    return lax.psum_scatter(partial_out.astype(jnp.bfloat16), "tp", scatter_dimension=1, tiled=True)


def solution(mesh):
    in_specs = (P("blk", "tp"), P(), P(None, "tp"), P("tp", None), P("blk", "tp"), P("blk", "tp"))
    out_specs = P("blk", "tp")
    return jax.shard_map(
        per_device, mesh=mesh, in_specs=in_specs, out_specs=out_specs, check_vma=False
    )
```

profile of v0, /device:TPU:0, one launch (start us, length us, event | category | flops | bytes accessed | tf_op | source)
XLA Modules:
  0.0 269.0 jit_solution(2074089705996655652)
XLA Ops:
  8.8 41.8 %all-gather.6.cloned.1.call-done = bf16[256,5120]{1,0:T(8,128)(2,1)} async-done(((bf16[256,2560]{1,0:T(8,128)(2,1)}), bf16[256,5120]{1,0:T(8,128)(2,1)}) %all-gather.6.cloned.1.call-update) | async-done | bytes 2621456 | tf_op jit(solution)/shard_map/all_gather | solution.py:24
  50.6 2.3 fusion.19
  53.0 4.5 %fusion.26 = bf16[256,384]{1,0:T(8,128)(2,1)S(1)} fusion(bf16[5120,384]{1,0:T(8,128)(2,1)} %param.10, bf16[256,5120]{1,0:T(8,128)(2,1)} %all-gather.6.cloned.1.call-done, f32[5120]{0:T(1024)} %param.9, f32[256]{0:T(256)S(1)} %add_rsqrt_fusion), kind=kOutput, calls=%fused_computation.31 | convolution fusion | flops 1011974144 | bytes 6771712 | tf_op jit(solution)/shard_map/dot_general | solution.py:27
  57.8 48.3 %all-gather.4.cloned.1.call-done = bf16[6144,384]{1,0:T(8,128)(2,1)} async-done(((bf16[384,384]{1,0:T(8,128)(2,1)}), bf16[6144,384]{1,0:T(8,128)(2,1)}) %all-gather.4.cloned.1.call-update) | async-done | bytes 4718608 | tf_op jit(solution)/shard_map/all_gather | solution.py:35
  106.1 13.0 %reshape.26 = bf16[4,1536,3,128]{3,2,1,0:T(4,128)(2,1)} reshape(bf16[6144,384]{1,0:T(8,128)(2,1)} %all-gather.4.cloned.1.call-done) | data formatting | bytes 9437184 | tf_op jit(solution)/shard_map/reshape | solution.py:39
  119.0 6.0 %copy.13 = bf16[4,1536,3,128]{3,1,2,0:T(8,128)(2,1)} copy(bf16[4,1536,3,128]{3,2,1,0:T(4,128)(2,1)} %reshape.26) | data formatting | bytes 9437184
  125.0 35.0 %all-gather.8.cloned.1.call-done = bf16[6144,384]{1,0:T(8,128)(2,1)} async-done(((bf16[384,384]{1,0:T(8,128)(2,1)}), bf16[6144,384]{1,0:T(8,128)(2,1)}) %all-gather.8.cloned.1.call-update) | async-done | bytes 4718608 | tf_op jit(solution)/shard_map/all_gather | solution.py:36
  160.1 12.9 %reshape.27 = bf16[4,1536,3,128]{3,2,1,0:T(4,128)(2,1)} reshape(bf16[6144,384]{1,0:T(8,128)(2,1)} %all-gather.8.cloned.1.call-done) | data formatting | bytes 9437184 | tf_op jit(solution)/shard_map/reshape | solution.py:40
  173.0 6.0 %copy.15 = bf16[4,1536,3,128]{3,1,2,0:T(8,128)(2,1)} copy(bf16[4,1536,3,128]{3,2,1,0:T(4,128)(2,1)} %reshape.27) | data formatting | bytes 9437184
  179.0 41.7 %while.15 = (s32[]{:T(128)}, f32[3,256]{1,0:T(4,128)S(1)}, f32[3,256]{1,0:T(4,128)S(1)}, f32[3,256,128]{2,1,0:T(8,128)S(1)}, bf16[4,1536,3,128]{3,1,2,0:T(8,128)...) while((s32[]{:T(128)}, f32[3,256]{1,0:T(4,128)S(1)}, ...), condition=%wide.region_4.5_spmd.clone, body=%wide.region_1.4_spmd.clone.sunk | while | flops 613715712 | bytes 36422788 | solution.py:61
  179.0 4.2 %bitcast_reduce_fusion.2 = (f32[3,256]{1,0:T(4,128)S(1)}, f32[3,1536,256]{2,1,0:T(8,128)}) fusion(bf16[256,3,128]{2,0,1:T(8,128)(2,1)S(1)} %get-tuple-element.175, bf16[4,1536,3,128]{3,1,2,0:T(8,128)(2,1)} %get-tuple-element.174, s32[]{:T(128)} %get-tuple-element.161), kind=kOutput, calls=%fused_computation.1.clone.1 | convolution fusion | flops 304348416 | bytes 6098432 | tf_op jit(solution)/shard_map/while/body/eval_jaxpr/qhd,khd->hqk/dot_general | solution.py:46
  183.2 3.3 %fusion.42 = f32[3,256]{1,0:T(4,128)S(1)} fusion(f32[3,1536,256]{2,1,0:T(8,128)} %get-tuple-element.149, f32[3,256]{1,0:T(4,128)S(1)} %select_maximum_fusion.2), kind=kLoop, calls=%fused_computation.4.clone.1 | loop fusion | flops 3538176 | bytes 4724736 | tf_op jit(solution)/shard_map/while/body/eval_jaxpr/reduce_sum | solution.py:52
  186.9 2.5 fusion.44
  189.4 4.2 %bitcast_reduce_fusion.2 = (f32[3,256]{1,0:T(4,128)S(1)}, f32[3,1536,256]{2,1,0:T(8,128)}) fusion(bf16[256,3,128]{2,0,1:T(8,128)(2,1)S(1)} %get-tuple-element.175, bf16[4,1536,3,128]{3,1,2,0:T(8,128)(2,1)} %get-tuple-element.174, s32[]{:T(128)} %get-tuple-element.161), kind=kOutput, calls=%fused_computation.1.clone.1 | convolution fusion | flops 304348416 | bytes 6098432 | tf_op jit(solution)/shard_map/while/body/eval_jaxpr/qhd,khd->hqk/dot_general | solution.py:46
  193.6 3.3 %fusion.42 = f32[3,256]{1,0:T(4,128)S(1)} fusion(f32[3,1536,256]{2,1,0:T(8,128)} %get-tuple-element.149, f32[3,256]{1,0:T(4,128)S(1)} %select_maximum_fusion.2), kind=kLoop, calls=%fused_computation.4.clone.1 | loop fusion | flops 3538176 | bytes 4724736 | tf_op jit(solution)/shard_map/while/body/eval_jaxpr/reduce_sum | solution.py:52
  197.3 2.5 fusion.44
  199.9 4.2 %bitcast_reduce_fusion.2 = (f32[3,256]{1,0:T(4,128)S(1)}, f32[3,1536,256]{2,1,0:T(8,128)}) fusion(bf16[256,3,128]{2,0,1:T(8,128)(2,1)S(1)} %get-tuple-element.175, bf16[4,1536,3,128]{3,1,2,0:T(8,128)(2,1)} %get-tuple-element.174, s32[]{:T(128)} %get-tuple-element.161), kind=kOutput, calls=%fused_computation.1.clone.1 | convolution fusion | flops 304348416 | bytes 6098432 | tf_op jit(solution)/shard_map/while/body/eval_jaxpr/qhd,khd->hqk/dot_general | solution.py:46
  204.0 3.3 %fusion.42 = f32[3,256]{1,0:T(4,128)S(1)} fusion(f32[3,1536,256]{2,1,0:T(8,128)} %get-tuple-element.149, f32[3,256]{1,0:T(4,128)S(1)} %select_maximum_fusion.2), kind=kLoop, calls=%fused_computation.4.clone.1 | loop fusion | flops 3538176 | bytes 4724736 | tf_op jit(solution)/shard_map/while/body/eval_jaxpr/reduce_sum | solution.py:52
  207.8 2.5 fusion.44
  210.3 4.2 %bitcast_reduce_fusion.2 = (f32[3,256]{1,0:T(4,128)S(1)}, f32[3,1536,256]{2,1,0:T(8,128)}) fusion(bf16[256,3,128]{2,0,1:T(8,128)(2,1)S(1)} %get-tuple-element.175, bf16[4,1536,3,128]{3,1,2,0:T(8,128)(2,1)} %get-tuple-element.174, s32[]{:T(128)} %get-tuple-element.161), kind=kOutput, calls=%fused_computation.1.clone.1 | convolution fusion | flops 304348416 | bytes 6098432 | tf_op jit(solution)/shard_map/while/body/eval_jaxpr/qhd,khd->hqk/dot_general | solution.py:46
  214.5 3.3 %fusion.42 = f32[3,256]{1,0:T(4,128)S(1)} fusion(f32[3,1536,256]{2,1,0:T(8,128)} %get-tuple-element.149, f32[3,256]{1,0:T(4,128)S(1)} %select_maximum_fusion.2), kind=kLoop, calls=%fused_computation.4.clone.1 | loop fusion | flops 3538176 | bytes 4724736 | tf_op jit(solution)/shard_map/while/body/eval_jaxpr/reduce_sum | solution.py:52
  218.2 2.5 fusion.44
  220.9 5.2 %convolution_convert_fusion = bf16[256,5120]{1,0:T(8,128)(2,1)} fusion(bf16[256,384]{0,1:T(8,128)(2,1)S(1)} %bitcast.40, bf16[384,5120]{1,0:T(8,128)(2,1)} %param.11), kind=kOutput, calls=%fused_computation.24 | convolution fusion | flops 1007943680 | bytes 6750208 | tf_op jit(solution)/shard_map/dot_general | solution.py:69
  226.1 36.4 %reduce-scatter.2.cloned.1.call-done = bf16[256,2560]{1,0:T(8,128)(2,1)} async-done(((bf16[256,5120]{1,0:T(8,128)(2,1)}), bf16[256,2560]{1,0:T(8,128)(2,1)}) %reduce-scatter.2.cloned.1.call-update) | async-done | bytes 1310736 | tf_op jit(solution)/shard_map/reduce_scatter | solution.py:70
  (36 shorter events, 4.7 us)
Async XLA Ops:
  6.5 44.1 %all-gather.6.cloned.1.call-start = ((), (), s32[]{:S(2)}) async-start(), calls=%async_computation.2 | async-start | bytes 3932160 | tf_op jit(solution)/shard_map/all_gather | solution.py:24
  7.3 98.8 %all-gather.4.cloned.1.call-start = ((), (), s32[]{:S(2)}) async-start(), calls=%async_computation.1 | async-start | bytes 5013504 | tf_op jit(solution)/shard_map/all_gather | solution.py:35
  8.0 152.0 %all-gather.8.cloned.1.call-start = ((), (), s32[]{:S(2)}) async-start(), calls=%async_computation.3 | async-start | bytes 5013504 | tf_op jit(solution)/shard_map/all_gather | solution.py:36
  8.7 253.8 %reduce-scatter.2.cloned.1.call-start = ((), (), s32[]{:S(2)}) async-start(), calls=%async_computation.4 | async-start | bytes 3932160 | tf_op jit(solution)/shard_map/reduce_scatter | solution.py:70
  183.1 3.8 %copy-start = (f32[3,1536,256]{2,1,0:T(8,128)S(1)}, f32[3,1536,256]{2,1,0:T(8,128)}, u32[]{:S(2)}) copy-start(f32[3,1536,256]{2,1,0:T(8,128)} %get-tuple-element.149) | copy-start | bytes 14155780 | tf_op jit(solution)/shard_map/while
  193.6 3.8 %copy-start = (f32[3,1536,256]{2,1,0:T(8,128)S(1)}, f32[3,1536,256]{2,1,0:T(8,128)}, u32[]{:S(2)}) copy-start(f32[3,1536,256]{2,1,0:T(8,128)} %get-tuple-element.149) | copy-start | bytes 14155780 | tf_op jit(solution)/shard_map/while
  204.0 3.8 %copy-start = (f32[3,1536,256]{2,1,0:T(8,128)S(1)}, f32[3,1536,256]{2,1,0:T(8,128)}, u32[]{:S(2)}) copy-start(f32[3,1536,256]{2,1,0:T(8,128)} %get-tuple-element.149) | copy-start | bytes 14155780 | tf_op jit(solution)/shard_map/while
  214.5 3.8 %copy-start = (f32[3,1536,256]{2,1,0:T(8,128)S(1)}, f32[3,1536,256]{2,1,0:T(8,128)}, u32[]{:S(2)}) copy-start(f32[3,1536,256]{2,1,0:T(8,128)} %get-tuple-element.149) | copy-start | bytes 14155780 | tf_op jit(solution)/shard_map/while
Sparse Core Ops, SparseCore 0:
  8.9 41.7 all-gather.5
  52.9 53.1 all-gather.3
  108.4 51.6 all-gather.7
  226.2 36.2 reduce-scatter.1
where the time goes:
time: 270 us; the launch traced here: 269 us
  waiting for transfers between devices  164 us (61%)
  local copies, waits for them, and re-layouts  40.2 us (15%)
  matrix products  36.3 us (13%)
  other arithmetic  15.6 us (6%)
  between operations  13.2 us (5%)
    all_gather x1, waiting for transfers between devices, per_device(): key_rows = lax.all_gather(enc_keys, 'blk', axis=0, tiled=True)  48.3 us
    all_gather x1, waiting for transfers between devices, per_device(): lax.all_gather(dec_states, 'tp', axis=1, tiled=True).astype(jnp.float32)  41.8 us
    reduce_scatter x1, waiting for transfers between devices, per_device(): lax.psum_scatter(partial_out.astype(jnp.bfloat16), 'tp', scatter_dimensio...  36.4 us
    all_gather x1, waiting for transfers between devices, per_device(): value_rows = lax.all_gather(enc_values, 'blk', axis=0, tiled=True)  35 us
    dot_general x4, matrix products, step_block(): jnp.einsum('qhd,khd->hqk', query_heads, key_block, preferred_element_type...  16.7 us
    reduce_sum x4, other arithmetic, step_block(): new_sum = row_sum * factor + jnp.sum(exp_scores, axis=2)  13.1 us
    reshape x1, local copies, waits for them, and re-layouts, per_device(): key_rows.reshape(count // width_rows, width_rows, heads, HEAD_DIM)  13 us
    reshape x1, local copies, waits for them, and re-layouts, per_device(): value_rows.reshape(count // width_rows, width_rows, heads, HEAD_DIM)  12.9 us
  transfers between devices with their start and end apart: 4, of which 4 were waited for; matrix products, arithmetic and copies ran while one was open for 10% of the time, Pallas kernels for 0%

commit v1 on v0

--- a/solution.py
+++ b/solution.py
@@ -21,7 +21,7 @@
     heads = query_weight.shape[1] // HEAD_DIM
     q_rows = dec_states.shape[0]
     score_scale = 1.0 / math.sqrt(HEAD_DIM)
-    states = lax.all_gather(dec_states, "tp", axis=1, tiled=True).astype(jnp.float32)
+    states = jnp.concatenate(lax.all_gather(dec_states, "tp"), axis=1).astype(jnp.float32)
     mean_sq = jnp.mean(states * states, axis=1, keepdims=True)
     normed = (states * lax.rsqrt(mean_sq + NORM_EPS) * norm_gain).astype(jnp.bfloat16)
     queries = jnp.dot(normed, query_weight, preferred_element_type=jnp.float32).astype(jnp.bfloat16)

time: 270 us -> 270 us (level)
  waiting for transfers between devices: 164 us -> 153 us
  other arithmetic: 15.6 us -> 22.8 us
  local copies, waits for them, and re-layouts: 40.2 us -> 46.2 us
  matrix products: 36.3 us -> 33.4 us
    all_gather x1, waiting for transfers between devices: 48.3 us -> 37.9 us  [per_device(): key_rows = lax.all_gather(enc_keys, 'blk', axis=0, tiled=True)]
    convert_element_type x0 -> x2, other arithmetic: none -> 8.96 us  [the longest x1 4.75 us: per_device(): jnp.concatenate(lax.all_gather(dec_states, 'tp'), axis=1)]
    convert_element_type x0 -> x1, local copies, waits for them, and re-layouts: none -> 6.05 us  [per_device(): jnp.concatenate(lax.all_gather(dec_states, 'tp'), axis=1)]
    dot_general x1, matrix products: 4.52 us -> 1.56 us  [per_device(): jnp.dot(normed, query_weight, preferred_element_type=jnp.float32)]
    unnamed x3 -> x9, local copies, waits for them, and re-layouts: 12.2 us -> 12.1 us
  transfers between devices with their start and end apart: 4 -> 4, of which waited for: 4 -> 4; matrix products, arithmetic and copies ran while one was open for 10% -> 14% of each run, Pallas kernels for 0% -> 0%
where the time goes in v1:
time: 270 us; the launch traced here: 269 us
  waiting for transfers between devices  153 us (57%)
  local copies, waits for them, and re-layouts  46.2 us (17%)
  matrix products  33.4 us (12%)
  other arithmetic  22.8 us (8%)
  between operations  13.2 us (5%)
    all_gather x1, waiting for transfers between devices, per_device(): lax.all_gather(dec_states, 'tp')  41.8 us
    all_gather x1, waiting for transfers between devices, per_device(): key_rows = lax.all_gather(enc_keys, 'blk', axis=0, tiled=True)  37.9 us
    reduce_scatter x1, waiting for transfers between devices, per_device(): lax.psum_scatter(partial_out.astype(jnp.bfloat16), 'tp', scatter_dimensio...  36.4 us
    all_gather x1, waiting for transfers between devices, per_device(): value_rows = lax.all_gather(enc_values, 'blk', axis=0, tiled=True)  35.1 us
    dot_general x4, matrix products, step_block(): jnp.einsum('qhd,khd->hqk', query_heads, key_block, preferred_element_type...  16.8 us
    reduce_sum x4, other arithmetic, step_block(): new_sum = row_sum * factor + jnp.sum(exp_scores, axis=2)  13.1 us
    reshape x1, local copies, waits for them, and re-layouts, per_device(): key_rows.reshape(count // width_rows, width_rows, heads, HEAD_DIM)  12.9 us
    reshape x1, local copies, waits for them, and re-layouts, per_device(): value_rows.reshape(count // width_rows, width_rows, heads, HEAD_DIM)  12.9 us
  transfers between devices with their start and end apart: 4, of which 4 were waited for; matrix products, arithmetic and copies ran while one was open for 14% of the time, Pallas kernels for 0%

profile of v1, /device:TPU:0, one launch (start us, length us, event | category | flops | bytes accessed | tf_op | source)
XLA Modules:
  0.0 269.2 jit_solution(13535137969171957085)
XLA Ops:
  8.8 41.8 %all-gather.9.cloned.1.call-done = bf16[512,2560]{1,0:T(8,128)(2,1)} async-done(((bf16[256,2560]{1,0:T(8,128)(2,1)}), bf16[512,2560]{1,0:T(8,128)(2,1)}) %all-gather.9.cloned.1.call-update) | async-done | bytes 2621456 | tf_op jit(solution)/shard_map/all_gather | solution.py:24
  50.6 4.8 %convert_bitcast_fusion = f32[256,2,2560]{2,0,1:T(8,128)} fusion(bf16[512,2560]{1,0:T(8,128)(2,1)} %all-gather.9.cloned.1.call-done), kind=kLoop, calls=%fused_computation.23 | loop fusion | flops 1310720 | bytes 7864320 | tf_op jit(solution)/shard_map/convert_element_type | solution.py:24
  55.4 6.1 %copy.19 = f32[256,2,2560]{0,2,1:T(8,128)} copy(f32[256,2,2560]{2,0,1:T(8,128)} %convert_bitcast_fusion) | data formatting | bytes 10485760 | tf_op jit(solution)/shard_map/convert_element_type | solution.py:24
  62.1 4.2 %fusion.21 = bf16[256,5120]{0,1:T(8,128)(2,1)S(1)} fusion(f32[256,2,2560]{0,2,1:T(8,128)} %copy.19, f32[5120]{0:T(1024)S(1)} %copy-done.2, f32[256]{0:T(256)S(1)} %add_rsqrt_fusion), kind=kLoop, calls=%fused_computation.28 | loop fusion | flops 3932160 | bytes 7885824 | tf_op jit(solution)/shard_map/convert_element_type | solution.py:26
  68.2 37.9 %all-gather.5.cloned.1.call-done = bf16[6144,384]{1,0:T(8,128)(2,1)} async-done(((bf16[384,384]{1,0:T(8,128)(2,1)}), bf16[6144,384]{1,0:T(8,128)(2,1)}) %all-gather.5.cloned.1.call-update) | async-done | bytes 4718608 | tf_op jit(solution)/shard_map/all_gather | solution.py:35
  106.1 12.9 %reshape.34 = bf16[4,1536,3,128]{3,2,1,0:T(4,128)(2,1)} reshape(bf16[6144,384]{1,0:T(8,128)(2,1)} %all-gather.5.cloned.1.call-done) | data formatting | bytes 9437184 | tf_op jit(solution)/shard_map/reshape | solution.py:39
  119.0 5.9 %copy.22 = bf16[4,1536,3,128]{3,1,2,0:T(8,128)(2,1)} copy(bf16[4,1536,3,128]{3,2,1,0:T(4,128)(2,1)} %reshape.34) | data formatting | bytes 9437184
  124.9 35.1 %all-gather.7.cloned.1.call-done = bf16[6144,384]{1,0:T(8,128)(2,1)} async-done(((bf16[384,384]{1,0:T(8,128)(2,1)}), bf16[6144,384]{1,0:T(8,128)(2,1)}) %all-gather.7.cloned.1.call-update) | async-done | bytes 4718608 | tf_op jit(solution)/shard_map/all_gather | solution.py:36
  160.1 12.9 %reshape.35 = bf16[4,1536,3,128]{3,2,1,0:T(4,128)(2,1)} reshape(bf16[6144,384]{1,0:T(8,128)(2,1)} %all-gather.7.cloned.1.call-done) | data formatting | bytes 9437184 | tf_op jit(solution)/shard_map/reshape | solution.py:40
  173.0 6.0 %copy.24 = bf16[4,1536,3,128]{3,1,2,0:T(8,128)(2,1)} copy(bf16[4,1536,3,128]{3,2,1,0:T(4,128)(2,1)} %reshape.35) | data formatting | bytes 9437184
  179.0 41.8 %while.15 = (s32[]{:T(128)}, f32[3,256]{1,0:T(4,128)S(1)}, f32[3,256]{1,0:T(4,128)S(1)}, f32[3,256,128]{2,1,0:T(8,128)S(1)}, bf16[4,1536,3,128]{3,1,2,0:T(8,128)...) while((s32[]{:T(128)}, f32[3,256]{1,0:T(4,128)S(1)}, ...), condition=%wide.region_4.5_spmd.clone, body=%wide.region_1.4_spmd.clone.sunk | while | flops 613715712 | bytes 36422788 | solution.py:61
  179.0 4.2 %bitcast_reduce_fusion.2 = (f32[3,256]{1,0:T(4,128)S(1)}, f32[3,1536,256]{2,1,0:T(8,128)}) fusion(bf16[256,3,128]{2,0,1:T(8,128)(2,1)S(1)} %get-tuple-element.182, bf16[4,1536,3,128]{3,1,2,0:T(8,128)(2,1)} %get-tuple-element.181, s32[]{:T(128)} %get-tuple-element.168), kind=kOutput, calls=%fused_computation.1.clone.1 | convolution fusion | flops 304348416 | bytes 6098432 | tf_op jit(solution)/shard_map/while/body/eval_jaxpr/qhd,khd->hqk/dot_general | solution.py:46
  183.2 3.3 %fusion.36 = f32[3,256]{1,0:T(4,128)S(1)} fusion(f32[3,1536,256]{2,1,0:T(8,128)} %get-tuple-element.156, f32[3,256]{1,0:T(4,128)S(1)} %select_maximum_fusion.2), kind=kLoop, calls=%fused_computation.4.clone.1 | loop fusion | flops 3538176 | bytes 4724736 | tf_op jit(solution)/shard_map/while/body/eval_jaxpr/reduce_sum | solution.py:52
  189.5 4.2 %bitcast_reduce_fusion.2 = (f32[3,256]{1,0:T(4,128)S(1)}, f32[3,1536,256]{2,1,0:T(8,128)}) fusion(bf16[256,3,128]{2,0,1:T(8,128)(2,1)S(1)} %get-tuple-element.182, bf16[4,1536,3,128]{3,1,2,0:T(8,128)(2,1)} %get-tuple-element.181, s32[]{:T(128)} %get-tuple-element.168), kind=kOutput, calls=%fused_computation.1.clone.1 | convolution fusion | flops 304348416 | bytes 6098432 | tf_op jit(solution)/shard_map/while/body/eval_jaxpr/qhd,khd->hqk/dot_general | solution.py:46
  193.7 3.3 %fusion.36 = f32[3,256]{1,0:T(4,128)S(1)} fusion(f32[3,1536,256]{2,1,0:T(8,128)} %get-tuple-element.156, f32[3,256]{1,0:T(4,128)S(1)} %select_maximum_fusion.2), kind=kLoop, calls=%fused_computation.4.clone.1 | loop fusion | flops 3538176 | bytes 4724736 | tf_op jit(solution)/shard_map/while/body/eval_jaxpr/reduce_sum | solution.py:52
  197.4 2.5 fusion.38
  199.9 4.2 %bitcast_reduce_fusion.2 = (f32[3,256]{1,0:T(4,128)S(1)}, f32[3,1536,256]{2,1,0:T(8,128)}) fusion(bf16[256,3,128]{2,0,1:T(8,128)(2,1)S(1)} %get-tuple-element.182, bf16[4,1536,3,128]{3,1,2,0:T(8,128)(2,1)} %get-tuple-element.181, s32[]{:T(128)} %get-tuple-element.168), kind=kOutput, calls=%fused_computation.1.clone.1 | convolution fusion | flops 304348416 | bytes 6098432 | tf_op jit(solution)/shard_map/while/body/eval_jaxpr/qhd,khd->hqk/dot_general | solution.py:46
  204.1 3.3 %fusion.36 = f32[3,256]{1,0:T(4,128)S(1)} fusion(f32[3,1536,256]{2,1,0:T(8,128)} %get-tuple-element.156, f32[3,256]{1,0:T(4,128)S(1)} %select_maximum_fusion.2), kind=kLoop, calls=%fused_computation.4.clone.1 | loop fusion | flops 3538176 | bytes 4724736 | tf_op jit(solution)/shard_map/while/body/eval_jaxpr/reduce_sum | solution.py:52
  207.9 2.5 fusion.38
  210.4 4.2 %bitcast_reduce_fusion.2 = (f32[3,256]{1,0:T(4,128)S(1)}, f32[3,1536,256]{2,1,0:T(8,128)}) fusion(bf16[256,3,128]{2,0,1:T(8,128)(2,1)S(1)} %get-tuple-element.182, bf16[4,1536,3,128]{3,1,2,0:T(8,128)(2,1)} %get-tuple-element.181, s32[]{:T(128)} %get-tuple-element.168), kind=kOutput, calls=%fused_computation.1.clone.1 | convolution fusion | flops 304348416 | bytes 6098432 | tf_op jit(solution)/shard_map/while/body/eval_jaxpr/qhd,khd->hqk/dot_general | solution.py:46
  214.6 3.3 %fusion.36 = f32[3,256]{1,0:T(4,128)S(1)} fusion(f32[3,1536,256]{2,1,0:T(8,128)} %get-tuple-element.156, f32[3,256]{1,0:T(4,128)S(1)} %select_maximum_fusion.2), kind=kLoop, calls=%fused_computation.4.clone.1 | loop fusion | flops 3538176 | bytes 4724736 | tf_op jit(solution)/shard_map/while/body/eval_jaxpr/reduce_sum | solution.py:52
  218.3 2.5 fusion.38
  221.0 5.2 %convolution_convert_fusion = bf16[256,5120]{1,0:T(8,128)(2,1)} fusion(bf16[256,384]{0,1:T(8,128)(2,1)S(1)} %bitcast.53, bf16[384,5120]{1,0:T(8,128)(2,1)} %param.11), kind=kOutput, calls=%fused_computation.24 | convolution fusion | flops 1007943680 | bytes 6750208 | tf_op jit(solution)/shard_map/dot_general | solution.py:69
  226.3 36.4 %reduce-scatter.2.cloned.1.call-done = bf16[256,2560]{1,0:T(8,128)(2,1)} async-done(((bf16[256,5120]{1,0:T(8,128)(2,1)}), bf16[256,2560]{1,0:T(8,128)(2,1)}) %reduce-scatter.2.cloned.1.call-update) | async-done | bytes 1310736 | tf_op jit(solution)/shard_map/reduce_scatter | solution.py:70
  (45 shorter events, 9.3 us)
Async XLA Ops:
  6.5 44.1 %all-gather.9.cloned.1.call-start = ((), (), s32[]{:S(2)}) async-start(), calls=%async_computation.4 | async-start | bytes 3932160 | tf_op jit(solution)/shard_map/all_gather | solution.py:24
  7.3 98.8 %all-gather.5.cloned.1.call-start = ((), (), s32[]{:S(2)}) async-start(), calls=%async_computation.1 | async-start | bytes 5013504 | tf_op jit(solution)/shard_map/all_gather | solution.py:35
  8.0 152.0 %all-gather.7.cloned.1.call-start = ((), (), s32[]{:S(2)}) async-start(), calls=%async_computation.2 | async-start | bytes 5013504 | tf_op jit(solution)/shard_map/all_gather | solution.py:36
  8.7 253.9 %reduce-scatter.2.cloned.1.call-start = ((), (), s32[]{:S(2)}) async-start(), calls=%async_computation.3 | async-start | bytes 3932160 | tf_op jit(solution)/shard_map/reduce_scatter | solution.py:70
  55.4 6.1 %copy-start.1 = (bf16[512,2560]{1,0:T(8,128)(2,1)S(1)}, bf16[512,2560]{1,0:T(8,128)(2,1)}, u32[]{:S(2)}) copy-start(bf16[512,2560]{1,0:T(8,128)(2,1)} %all-gather.9.cloned.1.call-done) | copy-start | bytes 7864324
  55.4 6.7 %copy-start.2 = (f32[5120]{0:T(1024)S(1)}, f32[5120]{0:T(1024)}, u32[]{:S(2)}) copy-start(f32[5120]{0:T(1024)} %param.9) | copy-start | bytes 61444
  61.4 4.8 %copy-start.3 = (bf16[5120,384]{1,0:T(8,128)(2,1)S(1)}, bf16[5120,384]{1,0:T(8,128)(2,1)}, u32[]{:S(2)}) copy-start(bf16[5120,384]{1,0:T(8,128)(2,1)} %param.10) | copy-start | bytes 11796484
  183.2 3.8 %copy-start = (f32[3,1536,256]{2,1,0:T(8,128)S(1)}, f32[3,1536,256]{2,1,0:T(8,128)}, u32[]{:S(2)}) copy-start(f32[3,1536,256]{2,1,0:T(8,128)} %get-tuple-element.156) | copy-start | bytes 14155780 | tf_op jit(solution)/shard_map/while
  193.6 3.8 %copy-start = (f32[3,1536,256]{2,1,0:T(8,128)S(1)}, f32[3,1536,256]{2,1,0:T(8,128)}, u32[]{:S(2)}) copy-start(f32[3,1536,256]{2,1,0:T(8,128)} %get-tuple-element.156) | copy-start | bytes 14155780 | tf_op jit(solution)/shard_map/while
  204.1 3.8 %copy-start = (f32[3,1536,256]{2,1,0:T(8,128)S(1)}, f32[3,1536,256]{2,1,0:T(8,128)}, u32[]{:S(2)}) copy-start(f32[3,1536,256]{2,1,0:T(8,128)} %get-tuple-element.156) | copy-start | bytes 14155780 | tf_op jit(solution)/shard_map/while
  214.6 3.8 %copy-start = (f32[3,1536,256]{2,1,0:T(8,128)S(1)}, f32[3,1536,256]{2,1,0:T(8,128)}, u32[]{:S(2)}) copy-start(f32[3,1536,256]{2,1,0:T(8,128)} %get-tuple-element.156) | copy-start | bytes 14155780 | tf_op jit(solution)/shard_map/while
Sparse Core Ops, SparseCore 0:
  8.9 41.7 all-gather.8
  52.9 53.1 all-gather.4
  108.4 51.6 all-gather.6
  226.4 36.2 reduce-scatter.1
